TPU v7x, 32 devices: a whole 2x2x4 slice. The times are simulated.
32 devices in a mesh: data: 32 (over z, y, x, core).
Axes of the slice: x: 2, y: 2, z: 4, core: 2. Of those that a mesh axis runs over, the one named last changes fastest.
Arguments:
- x_in: bfloat16 [256, 512, 1280], P('data')
- dy_out: bfloat16 [256, 512, 1280], P('data')
- lengths: int32 [128, 2], P('data')
- w_in: bfloat16 [1, 1280, 5120], replicated
- w_out: bfloat16 [1, 5120, 1280], replicated
Outputs:
- output 1: bfloat16 [1, 1280, 5120], replicated
- output 2: bfloat16 [1, 5120, 1280], replicated
- output 3: bfloat16 [256, 512, 1280], P('data')
All inputs are finite; a program needn't handle non-finite values.
Results may differ from a plain program's by a relative error of at most 0.0159579.
Values are sent between devices in bfloat16 or wider.
A program may use at most 1 GiB of HBM per device.

v0:
```python
import math
import jax
import jax.numpy as jnp
from jax import lax
from jax.sharding import PartitionSpec as P

GELU_SCALE = math.sqrt(2.0 / math.pi)
GELU_CUBIC = 0.044715


def gelu_value(pre_act):
    return 0.5 * pre_act * (1.0 + jnp.tanh(GELU_SCALE * (pre_act + GELU_CUBIC * pre_act * pre_act * pre_act)))


def gelu_slope(pre_act):
    inner = jnp.tanh(GELU_SCALE * (pre_act + GELU_CUBIC * pre_act * pre_act * pre_act))
    return 0.5 * (1.0 + inner) + 0.5 * pre_act * (1.0 - inner * inner) * GELU_SCALE * (1.0 + 3.0 * GELU_CUBIC * pre_act * pre_act)


def masked_grad(dy_rows, len_rows):
    positions = jnp.arange(dy_rows.shape[1], dtype=jnp.int32)
    keep = positions[None, :] < len_rows[:, None]
    return jnp.where(keep[:, :, None], dy_rows, jnp.zeros((), dy_rows.dtype)).reshape(-1, dy_rows.shape[2])


def forward_backward(x_rows, grad, w_in, w_out):
    layers = w_in.shape[0]
    hidden = x_rows
    saved = []
    for layer in range(layers):
        pre_act = jnp.dot(hidden, w_in[layer], preferred_element_type=jnp.float32).astype(jnp.bfloat16)
        act_out = gelu_value(pre_act.astype(jnp.float32)).astype(jnp.bfloat16)
        saved.append((hidden, pre_act, act_out))
        hidden = (hidden.astype(jnp.float32) + jnp.dot(act_out, w_out[layer], preferred_element_type=jnp.float32)).astype(jnp.bfloat16)
    grads_in = []
    grads_out = []
    for layer in reversed(range(layers)):
        hidden_in, pre_act, act_out = saved[layer]
        grads_out.append(jnp.einsum("tf,td->fd", act_out, grad, preferred_element_type=jnp.float32))
        d_act = jnp.einsum("td,fd->tf", grad, w_out[layer], preferred_element_type=jnp.float32)
        d_preact = (d_act * gelu_slope(pre_act.astype(jnp.float32))).astype(jnp.bfloat16)
        grads_in.append(jnp.einsum("td,tf->df", hidden_in, d_preact, preferred_element_type=jnp.float32))
        grad = (grad.astype(jnp.float32) + jnp.einsum("tf,df->td", d_preact, w_in[layer], preferred_element_type=jnp.float32)).astype(jnp.bfloat16)
    return grads_in[::-1], grads_out[::-1], grad


def solution(mesh):
    n_dev = mesh.shape["data"]

    def local_step(x_loc, dy_loc, len_loc, w_in, w_out):
        layers, d_model, d_ff = w_in.shape
        micro, rows = len_loc.shape
        seq_len = x_loc.shape[1]
        shard_len = d_model * d_ff // n_dev
        x_mb = x_loc.reshape(micro, rows * seq_len, d_model)
        dy_mb = dy_loc.reshape(micro, rows, seq_len, d_model)

        def step(carry, inputs):
            acc_in, acc_out = carry
            x_rows, dy_rows, len_rows = inputs
            grads_in, grads_out, dx_rows = forward_backward(x_rows, masked_grad(dy_rows, len_rows), w_in, w_out)
            new_in = []
            new_out = []
            for layer in range(layers):
                part_in = lax.psum_scatter(grads_in[layer].astype(jnp.bfloat16).reshape(n_dev, shard_len), "data", scatter_dimension=0, tiled=False)
                part_out = lax.psum_scatter(grads_out[layer].astype(jnp.bfloat16).reshape(n_dev, shard_len), "data", scatter_dimension=0, tiled=False)
                new_in.append(acc_in[layer] + part_in.astype(jnp.float32))
                new_out.append(acc_out[layer] + part_out.astype(jnp.float32))
            return (tuple(new_in), tuple(new_out)), dx_rows.reshape(rows, seq_len, d_model)

        zero_shard = jnp.zeros((shard_len,), jnp.float32)
        init = (tuple(zero_shard for layer in range(layers)), tuple(zero_shard for layer in range(layers)))
        sums, dx_all = lax.scan(step, init, (x_mb, dy_mb, len_loc))
        full_in = lax.all_gather(jnp.stack(sums[0]).astype(jnp.bfloat16), "data", axis=1, tiled=True)
        full_out = lax.all_gather(jnp.stack(sums[1]).astype(jnp.bfloat16), "data", axis=1, tiled=True)
        return full_in.reshape(layers, d_model, d_ff), full_out.reshape(layers, d_ff, d_model), dx_all.reshape(micro * rows, seq_len, d_model)

    return jax.shard_map(local_step, mesh=mesh, in_specs=(P("data"), P("data"), P("data"), P(), P()), out_specs=(P(), P(), P("data")), check_vma=False)
```

profile of v0, /device:TPU:0, one launch (start us, length us, event | category | flops | bytes accessed | tf_op | source)
XLA Modules:
  0.0 2379.3 jit_solution(5914465153815684263)
XLA Ops:
  9.4 2137.5 %while.15 = (s32[]{:T(128)}, f32[204800]{0:T(1024)}, f32[204800]{0:T(1024)}, bf16[4,2,512,1280]{3,2,1,0:T(8,128)(2,1)}, bf16[4,1024,1280]{2,1,0:T(8,128)(2,1)}, ...) while((s32[]{:T(128)}, f32[204800]{0:T(1024)}, ...), condition=%wide.region_3.4_spmd.clone, body=%wide.region_0.3_spmd.clone.sunk | while | flops 67305390080 | bytes 407147872 | solution.py:73
  12.8 20.8 fusion.63
  33.6 23.3 convolution_convert_fusion.5
  56.9 12.4 reshape.93
  69.3 28.6 %fusion.65 = bf16[1024,5120]{1,0:T(8,128)(2,1)} fusion(bf16[1024,5120]{1,0:T(8,128)(2,1)} %fusion.63, bf16[1024,1280]{1,0:T(8,128)(2,1)S(1)} %bitcast.66, bf16[1,5120,1280]{2,1,0:T(8,128)(2,1)} %get-tuple-element.225), kind=kOutput, calls=%fused_computation.13.clone.1 | convolution fusion | flops 13526630400 | bytes 36700160 | tf_op jit(solution)/shard_map/while/body/eval_jaxpr/td,fd->tf/dot_general | solution.py:40
  98.0 20.2 convolution_convert_fusion.4
  118.1 12.4 reshape.92
  132.2 20.2 add_convert_fusion.2
  154.1 384.3 %all-reduce.7.cloned.1.call-done = (bf16[32,204800]{1,0:T(8,128)(2,1)}, bf16[32,204800]{1,0:T(8,128)(2,1)}) async-done(((bf16[32,204800]{1,0:T(8,128)(2,1)}, bf16[32,204800]{1,0:T(8,128)(2,1)}), (bf16[32,204800]{1,0:T(8,128)(2,1)}, bf16[32,204800]{1,0:T(8,128)(2,1)})) %all-reduce.7.cloned.1.call-update) | async-done | bytes 26214416 | tf_op jit(solution)/shard_map/while
  538.4 2.3 dynamic-slice_convert_fusion.4
  540.7 2.3 dynamic-slice_convert_fusion.5
  548.8 20.8 fusion.63
  569.5 23.3 convolution_convert_fusion.5
  592.9 12.4 reshape.93
  605.3 28.6 %fusion.65 = bf16[1024,5120]{1,0:T(8,128)(2,1)} fusion(bf16[1024,5120]{1,0:T(8,128)(2,1)} %fusion.63, bf16[1024,1280]{1,0:T(8,128)(2,1)S(1)} %bitcast.66, bf16[1,5120,1280]{2,1,0:T(8,128)(2,1)} %get-tuple-element.225), kind=kOutput, calls=%fused_computation.13.clone.1 | convolution fusion | flops 13526630400 | bytes 36700160 | tf_op jit(solution)/shard_map/while/body/eval_jaxpr/td,fd->tf/dot_general | solution.py:40
  633.9 20.2 convolution_convert_fusion.4
  654.1 12.4 reshape.92
  668.2 20.2 add_convert_fusion.2
  690.1 381.0 %all-reduce.7.cloned.1.call-done = (bf16[32,204800]{1,0:T(8,128)(2,1)}, bf16[32,204800]{1,0:T(8,128)(2,1)}) async-done(((bf16[32,204800]{1,0:T(8,128)(2,1)}, bf16[32,204800]{1,0:T(8,128)(2,1)}), (bf16[32,204800]{1,0:T(8,128)(2,1)}, bf16[32,204800]{1,0:T(8,128)(2,1)})) %all-reduce.7.cloned.1.call-update) | async-done | bytes 26214416 | tf_op jit(solution)/shard_map/while
  1071.1 2.3 dynamic-slice_convert_fusion.4
  1073.4 2.3 dynamic-slice_convert_fusion.5
  1075.7 2.6 select_add_fusion.3
  1082.6 20.8 fusion.63
  1103.4 23.3 convolution_convert_fusion.5
  1126.7 12.4 reshape.93
  1139.1 28.6 %fusion.65 = bf16[1024,5120]{1,0:T(8,128)(2,1)} fusion(bf16[1024,5120]{1,0:T(8,128)(2,1)} %fusion.63, bf16[1024,1280]{1,0:T(8,128)(2,1)S(1)} %bitcast.66, bf16[1,5120,1280]{2,1,0:T(8,128)(2,1)} %get-tuple-element.225), kind=kOutput, calls=%fused_computation.13.clone.1 | convolution fusion | flops 13526630400 | bytes 36700160 | tf_op jit(solution)/shard_map/while/body/eval_jaxpr/td,fd->tf/dot_general | solution.py:40
  1167.8 20.2 convolution_convert_fusion.4
  1187.9 12.4 reshape.92
  1202.1 20.2 add_convert_fusion.2
  1223.9 381.0 %all-reduce.7.cloned.1.call-done = (bf16[32,204800]{1,0:T(8,128)(2,1)}, bf16[32,204800]{1,0:T(8,128)(2,1)}) async-done(((bf16[32,204800]{1,0:T(8,128)(2,1)}, bf16[32,204800]{1,0:T(8,128)(2,1)}), (bf16[32,204800]{1,0:T(8,128)(2,1)}, bf16[32,204800]{1,0:T(8,128)(2,1)})) %all-reduce.7.cloned.1.call-update) | async-done | bytes 26214416 | tf_op jit(solution)/shard_map/while
  1605.0 2.3 dynamic-slice_convert_fusion.4
  1607.2 2.3 dynamic-slice_convert_fusion.5
  1609.5 2.6 select_add_fusion.3
  1616.4 20.8 fusion.63
  1637.2 23.3 convolution_convert_fusion.5
  1660.6 12.4 reshape.93
  1673.0 28.6 %fusion.65 = bf16[1024,5120]{1,0:T(8,128)(2,1)} fusion(bf16[1024,5120]{1,0:T(8,128)(2,1)} %fusion.63, bf16[1024,1280]{1,0:T(8,128)(2,1)S(1)} %bitcast.66, bf16[1,5120,1280]{2,1,0:T(8,128)(2,1)} %get-tuple-element.225), kind=kOutput, calls=%fused_computation.13.clone.1 | convolution fusion | flops 13526630400 | bytes 36700160 | tf_op jit(solution)/shard_map/while/body/eval_jaxpr/td,fd->tf/dot_general | solution.py:40
  1701.6 20.2 convolution_convert_fusion.4
  1721.8 12.4 reshape.92
  1735.9 20.2 add_convert_fusion.2
  1757.8 381.0 %all-reduce.7.cloned.1.call-done = (bf16[32,204800]{1,0:T(8,128)(2,1)}, bf16[32,204800]{1,0:T(8,128)(2,1)}) async-done(((bf16[32,204800]{1,0:T(8,128)(2,1)}, bf16[32,204800]{1,0:T(8,128)(2,1)}), (bf16[32,204800]{1,0:T(8,128)(2,1)}, bf16[32,204800]{1,0:T(8,128)(2,1)})) %all-reduce.7.cloned.1.call-update) | async-done | bytes 26214416 | tf_op jit(solution)/shard_map/while
  2138.8 2.3 dynamic-slice_convert_fusion.4
  2141.0 2.3 dynamic-slice_convert_fusion.5
  2143.3 2.6 select_add_fusion.3
  2150.9 97.4 %all-gather.5.cloned.1.call-done = bf16[6553600]{0:T(1024)(128)(2,1)} async-done(((bf16[204800]{0:T(1024)(128)(2,1)}), bf16[6553600]{0:T(1024)(128)(2,1)}) %all-gather.5.cloned.1.call-update) | async-done | bytes 13107216 | tf_op jit(solution)/shard_map/all_gather | solution.py:74
  2248.2 19.5 reshape.77
  2267.7 79.4 %all-gather.7.cloned.1.call-done = bf16[6553600]{0:T(1024)(128)(2,1)} async-done(((bf16[204800]{0:T(1024)(128)(2,1)}), bf16[6553600]{0:T(1024)(128)(2,1)}) %all-gather.7.cloned.1.call-update) | async-done | bytes 13107216 | tf_op jit(solution)/shard_map/all_gather | solution.py:75
  2347.1 25.1 %reshape.78 = bf16[1,5120,1280]{2,1,0:T(8,128)(2,1)} reshape(bf16[6553600]{0:T(1024)(128)(2,1)} %all-gather.7.cloned.1.call-done) | data formatting | bytes 26214400 | tf_op jit(solution)/shard_map/reshape | solution.py:76
  (75 shorter events, 37.6 us)
Async XLA Ops:
  9.4 529.0 %all-reduce.7.cloned.1.call-start = ((), (), s32[]{:S(2)}) async-start(), calls=%async_computation.2 | async-start | bytes 52428800 | tf_op jit(solution)/shard_map/while
  12.8 20.8 copy-start
  130.5 1.7 copy-start.1
  132.2 410.7 %copy-start.2 = (f32[204800]{0:T(1024)S(1)}, f32[204800]{0:T(1024)}, u32[]{:S(2)}) copy-start(f32[204800]{0:T(1024)} %get-tuple-element.208) | copy-start | bytes 2457604 | tf_op jit(solution)/shard_map/while
  544.4 0.9 copy-start.3
  545.4 525.8 %all-reduce.7.cloned.1.call-start = ((), (), s32[]{:S(2)}) async-start(), calls=%async_computation.2 | async-start | bytes 52428800 | tf_op jit(solution)/shard_map/while
  548.7 20.8 copy-start
  666.5 1.7 copy-start.1
  668.2 407.4 %copy-start.2 = (f32[204800]{0:T(1024)S(1)}, f32[204800]{0:T(1024)}, u32[]{:S(2)}) copy-start(f32[204800]{0:T(1024)} %get-tuple-element.208) | copy-start | bytes 2457604 | tf_op jit(solution)/shard_map/while
  1078.3 0.9 copy-start.3
  1079.2 525.8 %all-reduce.7.cloned.1.call-start = ((), (), s32[]{:S(2)}) async-start(), calls=%async_computation.2 | async-start | bytes 52428800 | tf_op jit(solution)/shard_map/while
  1082.6 20.8 copy-start
  1200.3 1.7 copy-start.1
  1202.1 407.4 %copy-start.2 = (f32[204800]{0:T(1024)S(1)}, f32[204800]{0:T(1024)}, u32[]{:S(2)}) copy-start(f32[204800]{0:T(1024)} %get-tuple-element.208) | copy-start | bytes 2457604 | tf_op jit(solution)/shard_map/while
  1612.1 0.9 copy-start.3
  1613.0 525.7 %all-reduce.7.cloned.1.call-start = ((), (), s32[]{:S(2)}) async-start(), calls=%async_computation.2 | async-start | bytes 52428800 | tf_op jit(solution)/shard_map/while
  1616.4 20.8 copy-start
  1734.2 1.7 copy-start.1
  1735.9 407.4 %copy-start.2 = (f32[204800]{0:T(1024)S(1)}, f32[204800]{0:T(1024)}, u32[]{:S(2)}) copy-start(f32[204800]{0:T(1024)} %get-tuple-element.208) | copy-start | bytes 2457604 | tf_op jit(solution)/shard_map/while
  2145.9 0.9 copy-start.3
  2146.9 101.4 %all-gather.5.cloned.1.call-start = ((), (), s32[]{:S(2)}) async-start(), calls=%async_computation | async-start | bytes 13516800 | tf_op jit(solution)/shard_map/all_gather | solution.py:74
  2148.8 198.3 %all-gather.7.cloned.1.call-start = ((), (), s32[]{:S(2)}) async-start(), calls=%async_computation.1 | async-start | bytes 13516800 | tf_op jit(solution)/shard_map/all_gather | solution.py:75
Sparse Core Ops, SparseCore 0:
  130.6 407.7 all-reduce.6
  666.6 404.4 all-reduce.6
  1200.5 404.4 all-reduce.6
  1734.3 404.4 all-reduce.6
Sparse Core Ops, SparseCore 1:
  2150.8 97.4 all-gather.4
  2251.0 96.1 all-gather.6
where the time goes:
time: 2380 us
  waiting for transfers between devices  1700 us (71%)
  matrix products  452 us (19%)
  local copies, waits for them, and re-layouts  165 us (7%)
  other arithmetic  41.9 us (2%)
    while x8, waiting for transfers between devices  1530 us
    dot_general x4, matrix products, forward_backward(): jnp.einsum('td,fd->tf', grad, w_out[layer], preferred_element_type=jnp.fl...  115 us
    all_gather x1, waiting for transfers between devices, local_step(): lax.all_gather(jnp.stack(sums[0]).astype(jnp.bfloat16), 'data', axis=1, t...  97.4 us
    dot_general x4, matrix products, forward_backward(): jnp.einsum('tf,td->fd', act_out, grad, preferred_element_type=jnp.float32)  93.3 us
    dot_general x4, matrix products, forward_backward(): jnp.dot(hidden, w_in[layer], preferred_element_type=jnp.float32)  83.2 us
    dot_general x4, matrix products, forward_backward(): jnp.einsum('tf,df->td', d_preact, w_in[layer], preferred_element_type=jnp...  80.8 us
    dot_general x4, matrix products, forward_backward(): jnp.einsum('td,tf->df', hidden_in, d_preact, preferred_element_type=jnp.f...  80.7 us
    all_gather x1, waiting for transfers between devices, local_step(): lax.all_gather(jnp.stack(sums[1]).astype(jnp.bfloat16), 'data', axis=1, t...  79.4 us
  transfers between devices with their start and end apart: 6, of which 6 were waited for; matrix products, arithmetic and copies ran while one was open for 5% of the time, Pallas kernels for 0%

commit v1 on v0

v1 whole, which is shorter than its diff:
```python
import functools
import math
import jax
import jax.numpy as jnp
from jax import lax
from jax.experimental import pallas as pl
from jax.experimental.pallas import tpu as pltpu
from jax.sharding import PartitionSpec as P

GELU_SCALE = math.sqrt(2.0 / math.pi)
GELU_CUBIC = 0.044715
MESH = pl.DeviceIdType.MESH
NT = (((1,), (1,)), ((), ()))
TN = (((0,), (0,)), ((), ()))
f32 = jnp.float32
bf16 = jnp.bfloat16
ANY = pl.BlockSpec(memory_space=pl.ANY)

CHUNK = 256
STAGES = 5
EVENT_AT = (0, 1, 3, 5, 6, 7, 8, 9, 11, 13, 15)
LAG = 4


def gelu_both(u):
    sq = u * u
    half = 0.5 + 0.5 * jnp.tanh(u * (GELU_SCALE + (GELU_SCALE * GELU_CUBIC) * sq))
    slope = half + (u * (2.0 * GELU_SCALE + (6.0 * GELU_SCALE * GELU_CUBIC) * sq)) * (half * (1.0 - half))
    return u * half, slope


def part_table(d_model):
    rows = 1024 if d_model == 1280 else d_model // 2
    cols = 768 if d_model == 1280 else d_model // 2
    return (
        (0, 0, rows, 0, CHUNK, "cxyzw"),
        (0, rows, d_model - rows, 0, CHUNK, "czxyw"),
        (1, 0, CHUNK, 0, cols, "cyxzw"),
        (1, 0, CHUNK, cols, d_model - cols, "czyxw"),
    )


def grads_kernel(dims, len_ref, x_hbm, dy_hbm, w1_hbm, w2_hbm, o1_hbm, o2_hbm, du_hbm, *scratch):
    tokens, d_model, d_ff, seq = dims
    blocks = tokens // seq
    chunks = d_ff // CHUNK
    parts = part_table(d_model)
    (x_v, g_v, w1_v, w2_v, u0, u1, d0, d1, a_v, du_v, p1, p2) = scratch[:12]
    recv = [scratch[12 + 5 * k : 17 + 5 * k] for k in range(4)]
    (x_sem, g_sem, w_sem, du_sem, own_sem, rs_send, rs_recv, ag_send, ag_recv) = scratch[32:]

    me = lax.axis_index("data")
    weight = {"c": 1, "x": 2, "y": 4, "z": 8, "w": 16}
    bit = {k: lax.rem(lax.div(me, v), 2) for k, v in weight.items()}
    peer = {k: me + v * (1 - 2 * bit[k]) for k, v in weight.items()}

    barrier = pltpu.get_barrier_semaphore()
    for k in weight:
        pl.semaphore_signal(barrier, inc=1, device_id=(peer[k],), device_id_type=MESH)
    pl.semaphore_wait(barrier, STAGES)

    region, given = [], []
    for (_, r0, nr, c0, nc, order) in parts:
        mine, away = [(r0, nr, c0, nc)], []
        for s, name in enumerate(order):
            row, rows, col, cols = mine[-1]
            if s < STAGES - 1:
                half = rows // 2
                mine.append((row + bit[name] * half, half, col, cols))
                away.append((row + (1 - bit[name]) * half, half, col, cols))
            else:
                half = cols // 2
                mine.append((row, rows, col + bit[name] * half, half))
                away.append((row, rows, col + (1 - bit[name]) * half, half))
        region.append(mine)
        given.append(away)

    def cut(r):
        row, rows, col, cols = r
        row = row if isinstance(row, int) else pl.multiple_of(row, 16)
        col = col if isinstance(col, int) else pl.multiple_of(col, 128)
        return pl.ds(row, rows), pl.ds(col, cols)

    def partial(k, i, r):
        rows, cols = cut(r)
        return (p1, p2)[parts[k][0]].at[lax.rem(i, 3), rows, cols]

    def whole(k, i, r):
        row, rows, col, cols = r
        if parts[k][0] == 0:
            return o1_hbm.at[cut((row, rows, i * CHUNK + col, cols))]
        return o2_hbm.at[cut((i * CHUNK + row, rows, col, cols))]

    def reduce_copy(k, s, i):
        slot = lax.rem(i, 2)
        return pltpu.make_async_remote_copy(
            src_ref=partial(k, i, given[k][s]), dst_ref=recv[k][s].at[slot],
            send_sem=rs_send.at[slot, s, k], recv_sem=rs_recv.at[slot, s, k],
            device_id=(peer[parts[k][5][s]],), device_id_type=MESH)

    def gather_copy(k, s, i):
        slot = lax.rem(i, 2)
        r = region[k][s + 1]
        return pltpu.make_async_remote_copy(
            src_ref=partial(k, i, r) if s == STAGES - 1 else whole(k, i, r), dst_ref=whole(k, i, r),
            send_sem=ag_send.at[slot, s, k], recv_sem=ag_recv.at[slot, s, k],
            device_id=(peer[parts[k][5][s]],), device_id_type=MESH)

    def own_copy(k, i):
        r = region[k][STAGES]
        return pltpu.make_async_copy(partial(k, i, r), whole(k, i, r), own_sem.at[k])

    def event(e, i):
        for k in range(4):
            if 1 <= e <= STAGES:
                reduce_copy(k, e - 1, i).wait()
                rows, cols = cut(region[k][e])
                ref, slot = (p1, p2)[parts[k][0]], lax.rem(i, 3)
                ref[slot, rows, cols] = ref[slot, rows, cols] + recv[k][e - 1][lax.rem(i, 2)]
            if e < STAGES:
                reduce_copy(k, e, i).start()
            if e == STAGES:
                own_copy(k, i).start()
            if e > STAGES:
                gather_copy(k, 2 * STAGES - e, i).wait()
                if e == STAGES + 1:
                    own_copy(k, i).wait()
            if STAGES <= e < 2 * STAGES:
                gather_copy(k, 2 * STAGES - 1 - e, i).start()

    def events(i, point):
        for e in reversed(range(2 * STAGES + 1)):
            if EVENT_AT[e] % 4 == point:
                j = i - EVENT_AT[e] // 4 - (1 if point == 0 else 1)

                @pl.when((j >= 0) & (j < chunks))
                def _():
                    event(e, j)

    def weights(i):
        slot = lax.rem(i, 2)
        at = pl.ds(pl.multiple_of(i * CHUNK, CHUNK), CHUNK)
        return (pltpu.make_async_copy(w1_hbm.at[:, at], w1_v.at[slot], w_sem.at[slot, 0]),
                pltpu.make_async_copy(w2_hbm.at[at, :], w2_v.at[slot], w_sem.at[slot, 1]))

    def rows_of(b):
        return pl.ds(pl.multiple_of(b * seq, seq), seq)

    def loads(b):
        return (pltpu.make_async_copy(x_hbm.at[rows_of(b), :], x_v.at[rows_of(b), :], x_sem.at[b]),
                pltpu.make_async_copy(dy_hbm.at[rows_of(b), :], g_v.at[rows_of(b), :], g_sem.at[b]))

    def arrive(b):
        for copy in loads(b):
            copy.wait()
        keep = lax.broadcasted_iota(jnp.int32, (seq, d_model), 0) < len_ref[b]
        g_v[rows_of(b), :] = jnp.where(keep, g_v[rows_of(b), :], jnp.zeros((), bf16))

    def dots(b, slot, u, d):
        u[...] = jnp.dot(x_v[rows_of(b), :], w1_v[slot], preferred_element_type=f32).astype(bf16)
        d[...] = lax.dot_general(g_v[rows_of(b), :], w2_v[slot], NT, preferred_element_type=f32)

    def pointwise(b, u, d):
        a, slope = gelu_both(u[...].astype(f32))
        a_v[rows_of(b), :] = a.astype(bf16)
        du_v[rows_of(b), :] = (d[...] * slope).astype(bf16)

    def du_out(i):
        return pltpu.make_async_copy(du_v, du_hbm.at[:, pl.ds(pl.multiple_of(i * CHUNK, CHUNK), CHUNK)], du_sem)

    for copy in weights(0):
        copy.start()
    for b in range(blocks):
        for copy in loads(b):
            copy.start()
    for copy in weights(0):
        copy.wait()
    arrive(0)
    dots(0, 0, u0, d0)

    @pl.loop(0, chunks + LAG)
    def _(i):
        busy = i < chunks
        slot = lax.rem(i, 2)

        @pl.when(i + 1 < chunks)
        def _():
            for copy in weights(i + 1):
                copy.start()

        @pl.when((i > 0) & (i <= chunks))
        def _():
            du_out(i - 1).wait()

        @pl.loop(0, 2)
        def _(half):
            @pl.when(busy)
            def _():
                @pl.loop(0, blocks // 4)
                def _(pair):
                    b = half * (blocks // 2) + pair * 2
                    last = b + 2 >= blocks

                    @pl.when(i == 0)
                    def _():
                        arrive(b + 1)

                        @pl.when(jnp.logical_not(last))
                        def _():
                            arrive(b + 2)

                    @pl.when(last & (i + 1 < chunks))
                    def _():
                        for copy in weights(i + 1):
                            copy.wait()

                    pointwise(b, u0, d0)
                    dots(b + 1, slot, u1, d1)
                    pointwise(b + 1, u1, d1)
                    dots(lax.rem(b + 2, blocks), lax.rem(slot + last.astype(jnp.int32), 2), u0, d0)

            @pl.when(half == 0)
            def _():
                events(i, 1)

            @pl.when((half == 1) & busy)
            def _():
                du_out(i).start()

        events(i, 2)
        third = lax.rem(i, 3)

        @pl.when(busy)
        def _():
            p2[third] = lax.dot_general(a_v[...], g_v[...], TN, preferred_element_type=f32).astype(bf16)

        events(i, 3)

        @pl.when(busy)
        def _():
            p1[third] = lax.dot_general(x_v[...], du_v[...], TN, preferred_element_type=f32).astype(bf16)

        events(i + 1, 0)


def grads_call(dims, lens, x, dy, w1, w2):
    tokens, d_model, d_ff, seq = dims
    scratch = [
        pltpu.VMEM((tokens, d_model), bf16), pltpu.VMEM((tokens, d_model), bf16),
        pltpu.VMEM((2, d_model, CHUNK), bf16), pltpu.VMEM((2, CHUNK, d_model), bf16),
        pltpu.VMEM((seq, CHUNK), bf16), pltpu.VMEM((seq, CHUNK), bf16),
        pltpu.VMEM((seq, CHUNK), f32), pltpu.VMEM((seq, CHUNK), f32),
        pltpu.VMEM((tokens, CHUNK), bf16), pltpu.VMEM((tokens, CHUNK), bf16),
        pltpu.VMEM((3, d_model, CHUNK), bf16), pltpu.VMEM((3, CHUNK, d_model), bf16),
    ]
    for (_, _, rows, _, cols, _) in part_table(d_model):
        for s in range(STAGES):
            last = s == STAGES - 1
            scratch.append(pltpu.VMEM((2, rows >> (4 if last else s + 1), cols // 2 if last else cols), bf16))
    dma = pltpu.SemaphoreType.DMA
    scratch += [dma((tokens // seq,)), dma((tokens // seq,)), dma((2, 2)), dma, dma((4,))]
    scratch += [dma((2, STAGES, 4))] * 4
    flops = 8 * tokens * d_model * d_ff
    return pl.pallas_call(
        functools.partial(grads_kernel, dims),
        out_shape=[jax.ShapeDtypeStruct((d_model, d_ff), bf16), jax.ShapeDtypeStruct((d_ff, d_model), bf16),
                   jax.ShapeDtypeStruct((tokens, d_ff), bf16)],
        in_specs=[pl.BlockSpec(memory_space=pltpu.SMEM)] + [ANY] * 4,
        out_specs=[ANY] * 3,
        scratch_shapes=scratch,
        compiler_params=pltpu.CompilerParams(collective_id=0, has_side_effects=True, vmem_limit_bytes=62 * 2**20),
        cost_estimate=pl.CostEstimate(flops=flops, bytes_accessed=2 * tokens * d_ff, transcendentals=tokens * d_ff),
        name="grads",
    )(lens, x, dy, w1, w2)


def finish_kernel(dims, len_ref, o1_hbm, o2_hbm, du_hbm, dy_hbm, w1_hbm, g1_hbm, g2_hbm, dx_hbm,
                  w1_v, du_v, g_v, dx_v, c1_v, c2_v, w_sem, in_sem, out_sem, c_in, c_out):
    tokens, d_model, d_ff, seq, block = dims
    steps = tokens // block
    per_seq = seq // block
    n1, n2 = d_model // steps, d_ff // steps

    def rows(b, n):
        return pl.ds(pl.multiple_of(b * n, n), n)

    def valid(b):
        return len_ref[lax.div(b, per_seq)] > lax.rem(b, per_seq) * block

    def ins(b):
        slot = lax.rem(b, 2)
        return (pltpu.make_async_copy(du_hbm.at[rows(b, block), :], du_v.at[slot], in_sem.at[slot, 0]),
                pltpu.make_async_copy(dy_hbm.at[rows(b, block), :], g_v.at[slot], in_sem.at[slot, 1]))

    def out(b):
        slot = lax.rem(b, 2)
        return pltpu.make_async_copy(dx_v.at[slot], dx_hbm.at[rows(b, block), :], out_sem.at[slot])

    def carry_in(b):
        slot = lax.rem(b, 2)
        return (pltpu.make_async_copy(o1_hbm.at[rows(b, n1), :], c1_v.at[slot], c_in.at[slot, 0]),
                pltpu.make_async_copy(o2_hbm.at[rows(b, n2), :], c2_v.at[slot], c_in.at[slot, 1]))

    def carry_out(b):
        slot = lax.rem(b, 2)
        return (pltpu.make_async_copy(c1_v.at[slot], g1_hbm.at[rows(b, n1), :], c_out.at[slot, 0]),
                pltpu.make_async_copy(c2_v.at[slot], g2_hbm.at[rows(b, n2), :], c_out.at[slot, 1]))

    def fetch(b):
        @pl.when(valid(b))
        def _():
            for copy in ins(b):
                copy.start()

    fetch(0)
    load_w = pltpu.make_async_copy(w1_hbm, w1_v, w_sem)
    load_w.start()
    for copy in carry_in(0):
        copy.start()
    load_w.wait()

    @pl.loop(0, steps)
    def _(b):
        slot = lax.rem(b, 2)

        @pl.when(b + 1 < steps)
        def _():
            fetch(b + 1)

        @pl.when(b > 0)
        def _():
            for copy in carry_out(b - 1):
                copy.wait()

        @pl.when(b + 1 < steps)
        def _():
            for copy in carry_in(b + 1):
                copy.start()

        for copy in carry_in(b):
            copy.wait()
        for copy in carry_out(b):
            copy.start()

        @pl.when(b > 1)
        def _():
            out(b - 2).wait()

        @pl.when(valid(b))
        def _():
            for copy in ins(b):
                copy.wait()
            first = lax.rem(b, per_seq) * block
            keep = first + lax.broadcasted_iota(jnp.int32, (block, d_model), 0) < len_ref[lax.div(b, per_seq)]
            g = jnp.where(keep, g_v[slot], jnp.zeros((), bf16)).astype(f32)
            dx_v[slot] = (g + lax.dot_general(du_v[slot], w1_v[...], NT, preferred_element_type=f32)).astype(bf16)

        @pl.when(jnp.logical_not(valid(b)))
        def _():
            dx_v[slot] = jnp.zeros((block, d_model), bf16)

        out(b).start()

    for copy in carry_out(steps - 1):
        copy.wait()
    out(steps - 2).wait()
    out(steps - 1).wait()


def finish_call(dims, lens, o1, o2, du, dy, w1):
    tokens, d_model, d_ff, seq, block = dims
    steps = tokens // block
    dma = pltpu.SemaphoreType.DMA
    return pl.pallas_call(
        functools.partial(finish_kernel, dims),
        out_shape=[jax.ShapeDtypeStruct((d_model, d_ff), bf16), jax.ShapeDtypeStruct((d_ff, d_model), bf16),
                   jax.ShapeDtypeStruct((tokens, d_model), bf16)],
        in_specs=[pl.BlockSpec(memory_space=pltpu.SMEM)] + [ANY] * 5,
        out_specs=[ANY] * 3,
        scratch_shapes=[
            pltpu.VMEM((d_model, d_ff), bf16), pltpu.VMEM((2, block, d_ff), bf16), pltpu.VMEM((2, block, d_model), bf16),
            pltpu.VMEM((2, block, d_model), bf16), pltpu.VMEM((2, d_model // steps, d_ff), bf16),
            pltpu.VMEM((2, d_ff // steps, d_model), bf16), dma, dma((2, 2)), dma((2,)), dma((2, 2)), dma((2, 2))],
        compiler_params=pltpu.CompilerParams(vmem_limit_bytes=62 * 2**20),
        cost_estimate=pl.CostEstimate(flops=2 * tokens * d_model * d_ff, bytes_accessed=2 * tokens * d_ff, transcendentals=0),
        name="finish",
    )(lens, o1, o2, du, dy, w1)


def solution(mesh):
    def local_step(x_loc, dy_loc, len_loc, w_in, w_out):
        layers, d_model, d_ff = w_in.shape
        rows, seq, _ = x_loc.shape
        tokens = rows * seq
        lens = len_loc.reshape(rows)
        x, dy = x_loc.reshape(tokens, d_model), dy_loc.reshape(tokens, d_model)
        w1, w2 = w_in.reshape(d_model, d_ff), w_out.reshape(d_ff, d_model)
        o1, o2, du = grads_call((tokens, d_model, d_ff, seq), lens, x, dy, w1, w2)
        g1, g2, dx = finish_call((tokens, d_model, d_ff, seq, seq // 2), lens, o1, o2, du, dy, w1)
        return g1.reshape(layers, d_model, d_ff), g2.reshape(layers, d_ff, d_model), dx.reshape(rows, seq, d_model)

    return jax.shard_map(local_step, mesh=mesh, in_specs=(P("data"), P("data"), P("data"), P(), P()), out_specs=(P(), P(), P("data")), check_vma=False)
```

time: 2380 us -> 414 us (0.17)
  waiting for transfers between devices: 1700 us -> 0 us
  matrix products: 452 us -> 0 us
  Pallas kernels: 0 us -> 409 us
  local copies, waits for them, and re-layouts: 165 us -> 1.39 us
  other arithmetic: 41.9 us -> 0 us
    while x8 -> x0, waiting for transfers between devices: 1530 us -> none
    dot_general x20 -> x0, matrix products: 452 us -> none  [the longest x4 115 us: forward_backward(): jnp.einsum('td,fd->tf', grad, w_out[layer], preferred_element_type=jnp.fl...]
    pallas_call x0 -> x2, Pallas kernels: none -> 409 us  [the longest x1 347 us: grads_call(): pl.pallas_call(functools.partial(grads_kernel, dims), out_shape=[jax.Shap...]
    all_gather x2 -> x0, waiting for transfers between devices: 177 us -> none  [the longest x1 97.4 us: local_step(): lax.all_gather(jnp.stack(sums[0]).astype(jnp.bfloat16), 'data', axis=1, t...]
    reshape x10 -> x1, local copies, waits for them, and re-layouts: 144 us -> 0.63 us  [local_step(): lens = len_loc.reshape(rows)]
  transfers between devices with their start and end apart: 6 -> 0, of which waited for: 6 -> 0; matrix products, arithmetic and copies ran while one was open for 5% -> 0% of each run, Pallas kernels for 0% -> 0%
where the time goes in v1:
time: 414 us; the launch traced here: 412 us
  Pallas kernels  409 us (99%)
    pallas_call x1, Pallas kernels, grads_call(): pl.pallas_call(functools.partial(grads_kernel, dims), out_shape=[jax.Shap...  347 us
    pallas_call x1, Pallas kernels, finish_call(): pl.pallas_call(functools.partial(finish_kernel, dims), out_shape=[jax.Sha...  62.5 us

profile of v1, /device:TPU:0, one launch (start us, length us, event | category | flops | bytes accessed | tf_op | source)
XLA Modules:
  0.0 411.5 jit_solution(16705499570772347852)
XLA Ops:
  0.6 0.8 copy.9
  1.4 0.6 reshape.30.len_ref
  2.0 347.0 %grads.1 = (bf16[1280,5120]{1,0:T(8,128)(2,1)}, bf16[5120,1280]{1,0:T(8,128)(2,1)}, bf16[4096,5120]{1,0:T(8,128)(2,1)}) custom-call(s32[8]{0:T(128)} %reshape.30.len_ref, bf16[4096,1280]{1,0:T(8,128)(2,1)} %bitcast.10, bf16[4096,1280]{1,0:T(8,128)(2,1)} %bitcast.11, bf16[1280,5120]{1,0:T(8,128)(2,1)} %bitcast.8, bf16[5120,1280]{1,0:T(8,128)(2,1)} %bitcast.7), custom_call_target="tpu_custom_call" | custom-call | flops 214748364800 | bytes 41943040 | tf_op jit(solution)/shard_map/grads/pallas_call | solution.py:264
  349.0 62.5 %finish.1 = (bf16[1280,5120]{1,0:T(8,128)(2,1)}, bf16[5120,1280]{1,0:T(8,128)(2,1)}, bf16[4096,1280]{1,0:T(8,128)(2,1)}) custom-call(s32[8]{0:T(128)} %reshape.30.len_ref, bf16[1280,5120]{1,0:T(8,128)(2,1)} %get-tuple-element.9.o1_hbm, bf16[5120,1280]{1,0:T(8,128)(2,1)} %get-tuple-element.10.o2_hbm, bf16[4096,5120]{1,0:T(8,128)(2,1)} %get-tuple-element.11.du_hbm, ...), custom_call_target="tpu_custom_call" | custom-call | flops 53687091200 | bytes 41943040 | tf_op jit(solution)/shard_map/finish/pallas_call | solution.py:374
